TPU v7x, 256 devices: a 4x2x16 block of a 4x16x16 slice. The times are simulated.
256 devices in a mesh: groups: 2 (over y), context: 128 (over x, z, core).
Axes of the slice: x: 4, y: 2, z: 16, core: 2. Of those that a mesh axis runs over, the one named last changes fastest.
The devices are a block of a 4x16x16 slice.
Arguments:
- query_proj: bfloat16 [32768, 5120], P(('groups', 'context')), parts along dimension 0, may hold values from -100 to 100
- key_proj: bfloat16 [32768, 1024], P(('groups', 'context')), parts along dimension 0, may hold values from -100 to 100
- values: bfloat16 [32768, 1024], P(('groups', 'context')), parts along dimension 0, may hold values from -6 to 6
- grad_out: bfloat16 [32768, 5120], P(('groups', 'context')), parts along dimension 0, may hold values from -6 to 6
- query_gain: float32 [5120], replicated, may hold values from 0.1 to 1.9
- key_gain: float32 [1024], replicated, may hold values from 0.1 to 1.9
- segments: int32 [32768], P('groups'), parts along dimension 0, may hold values from 0 to 63, never falling along the last dimension, each value on 1 to 512 neighbouring positions
- layout: int32 [512], P('groups'), parts along dimension 0, may hold values from 0 to 255, as said below
Outputs:
- query_grad: bfloat16 [32768, 5120], P(('groups', 'context')), parts along dimension 0
- key_grad: bfloat16 [32768, 1024], P(('groups', 'context')), parts along dimension 0
- value_grad: bfloat16 [32768, 1024], P(('groups', 'context')), parts along dimension 0
- query_gain_grad: float32 [10240], P('groups'), parts along dimension 0
- key_gain_grad: float32 [2048], P('groups'), parts along dimension 0
There are 2 independent parts, one for each index of `groups`. A program takes and returns all parts, laid end to end along the dimension named above; an argument that names none is the same for every part. Nothing has to cross between parts.
Inputs may be any that keep to these rules, and one draw needn't show every extreme that they name: layout is a permutation of the spans; slots are ordered device by device, 2 to a device, and each aligned run of 8 slots holds the spans of one sequence of 512 positions in some order. `segments`: document numbers never fall along the stream; a document has 1 to 512 positions, and one has exactly 512.
All inputs are finite; a program needn't handle non-finite values.
Results may differ from a plain program's by a relative error of at most 0.0086.
Values may be sent and summed in bfloat16 or wider, within the bound.
A program may use at most 128 MiB of HBM per device.

v0:
```python
import jax
import jax.numpy as jnp
from jax import lax
from jax.sharding import Mesh
from jax.sharding import PartitionSpec as P

QUERY_HEADS = 40
KEY_VALUE_HEADS = 8
HEAD_SIZE = 128
SPAN = 64
SEQ_BITS = 2
SEQ_DEVS = 4
LENGTH = 512
CONTEXT = ("context_0", "context_1", "context_2")
GROUPS_CONTEXT = ("groups", "context_0", "context_1", "context_2")
NORM_EPS = 1e-06
ROPE_BASE = 500000.0


def swapped(block, axis, apart):
    count = lax.axis_size(axis)
    route = []
    for low in range(count):
        high = low | 1 << apart
        if high != low and high < count:
            route += [(low, high), (high, low)]
    return lax.ppermute(block, axis, route)


def for_sending(array):

    def short(part):
        return part.astype(jnp.bfloat16) if part.dtype == jnp.float32 else part

    return jax.tree.map(short, array)


def by_axis(array, axes):
    for axis in axes:
        array = lax.psum(array, axis)
    return array


def rope_angles(positions, head_dim):
    half_dim = head_dim // 2
    inv_freq = jnp.power(ROPE_BASE, -2.0 * jnp.arange(half_dim, dtype=jnp.float32) / head_dim)
    angles = positions.astype(jnp.float32)[:, None] * inv_freq[None, :]
    return (jnp.cos(angles), jnp.sin(angles))


def rotate(inputs, cosine, sine, sign_flip):
    tok_rows = inputs.shape[0]
    half_dim = cosine.shape[1]
    halves = inputs.reshape(tok_rows, inputs.shape[1] // (2 * half_dim), 2, half_dim)
    lower_half = halves[:, :, 0]
    upper_half = halves[:, :, 1]
    cosine_b = cosine[:, None, :]
    sine_b = sine[:, None, :] * sign_flip
    rotated = jnp.stack(
        [lower_half * cosine_b - upper_half * sine_b, upper_half * cosine_b + lower_half * sine_b],
        axis=2,
    )
    return rotated.reshape(tok_rows, inputs.shape[1])


def norm_forward(inputs, gain_row):
    mean_sq = jnp.mean(inputs * inputs, axis=1, keepdims=True)
    factor = lax.rsqrt(mean_sq + NORM_EPS)
    return (inputs * factor * gain_row[None, :], factor)


def norm_backward(inputs, factor, gain_row, upstream):
    weighted = upstream * gain_row[None, :]
    inner_sum = jnp.mean(weighted * inputs, axis=1, keepdims=True)
    grad_in = factor * weighted - inputs * factor * factor * factor * inner_sum
    return (grad_in, jnp.sum(upstream * inputs * factor, axis=0))


def head_gradients(queries, key_rows, value_rows, grad_rows, allowed, query_head_group, head_dim):
    tok_rows = queries.shape[0]
    factor = head_dim ** (-0.5)
    query_heads = queries.reshape(tok_rows, query_head_group, head_dim)
    grad_heads = grad_rows.reshape(tok_rows, query_head_group, head_dim)
    scores = (
        jnp.einsum("qgd,kd->gqk", query_heads, key_rows, preferred_element_type=jnp.float32)
        * factor
    )
    scores = jnp.where(allowed[None], scores, -jnp.inf)
    row_max = jnp.max(scores, axis=2, keepdims=True)
    expo = jnp.exp(scores - row_max)
    attn_probs = expo / jnp.sum(expo, axis=2, keepdims=True)
    dprobs = jnp.einsum("qgd,kd->gqk", grad_heads, value_rows, preferred_element_type=jnp.float32)
    row_delta = jnp.sum(attn_probs * dprobs, axis=2, keepdims=True)
    dscores = (attn_probs * (dprobs - row_delta)).astype(jnp.bfloat16)
    probs_low = attn_probs.astype(jnp.bfloat16)
    query_part = (
        jnp.einsum("gqk,kd->qgd", dscores, key_rows, preferred_element_type=jnp.float32) * factor
    )
    key_part = (
        jnp.einsum("gqk,qgd->kd", dscores, query_heads, preferred_element_type=jnp.float32) * factor
    )
    value_part = jnp.einsum(
        "gqk,qgd->kd", probs_low, grad_heads, preferred_element_type=jnp.float32
    )
    return (query_part.reshape(tok_rows, query_head_group * head_dim), key_part, value_part)


def token_info(devices, tok_rows, layout, segments):
    local_index = jnp.arange(tok_rows, dtype=jnp.int32)
    slot_ids = devices[:, None] * (tok_rows // SPAN) + local_index[None, :] // SPAN
    positions = jnp.take(layout, slot_ids) * SPAN + local_index[None, :] % SPAN
    positions = positions.reshape(-1)
    return (positions, jnp.take(segments, positions))


def body(query_proj, key_proj, values, grad_out, query_gain, key_gain, segments, layout):
    tok_rows = query_proj.shape[0]
    my_index = lax.axis_index(CONTEXT)
    query_head_group = QUERY_HEADS // KEY_VALUE_HEADS
    group_width = query_head_group * HEAD_SIZE
    local_rank = my_index % SEQ_DEVS
    seq_base = my_index - local_rank
    positions, doc_query = token_info(jnp.reshape(my_index, (1,)), tok_rows, layout, segments)
    cosine, sine = rope_angles(positions % LENGTH, HEAD_SIZE)
    q_inputs = query_proj.astype(jnp.float32)
    k_inputs = key_proj.astype(jnp.float32)
    q_normed, q_factor = norm_forward(q_inputs, query_gain)
    k_normed, k_factor = norm_forward(k_inputs, key_gain)
    q_rope = rotate(q_normed, cosine, sine, 1.0).astype(jnp.bfloat16)
    k_rope = rotate(k_normed, cosine, sine, 1.0).astype(jnp.bfloat16)
    bit_order = list(range(SEQ_BITS))
    held_k, held_v = (k_rope, values)
    owners = jnp.reshape(local_rank, (1,))
    for bit in bit_order:
        got_k, got_v = swapped((held_k, held_v), CONTEXT, bit)
        held_k = jnp.concatenate([held_k, got_k], axis=0)
        held_v = jnp.concatenate([held_v, got_v], axis=0)
        owners = jnp.concatenate([owners, jnp.bitwise_xor(owners, 1 << bit)])
    pos_key, doc_key = token_info(seq_base + owners, tok_rows, layout, segments)
    allowed = (doc_key[None, :] == doc_query[:, None]) & (pos_key[None, :] <= positions[:, None])
    query_parts, key_parts, value_parts = ([], [], [])
    for key_value_head in range(KEY_VALUE_HEADS):
        query_part, key_part, value_part = head_gradients(
            q_rope[:, key_value_head * group_width : (key_value_head + 1) * group_width],
            held_k[:, key_value_head * HEAD_SIZE : (key_value_head + 1) * HEAD_SIZE],
            held_v[:, key_value_head * HEAD_SIZE : (key_value_head + 1) * HEAD_SIZE],
            grad_out[:, key_value_head * group_width : (key_value_head + 1) * group_width],
            allowed,
            query_head_group,
            HEAD_SIZE,
        )
        query_parts.append(query_part)
        key_parts.append(key_part)
        value_parts.append(value_part)
    dq_rope = jnp.concatenate(query_parts, axis=1)
    dk_all = jnp.concatenate(key_parts, axis=1)
    dv_all = jnp.concatenate(value_parts, axis=1)
    dq_normed = rotate(dq_rope, cosine, sine, -1.0)
    query_grad, q_gain_part = norm_backward(q_inputs, q_factor, query_gain, dq_normed)
    for bit in reversed(bit_order):
        half_rows = dk_all.shape[0] // 2
        back_k, back_v = swapped(
            (for_sending(dk_all[half_rows:]), for_sending(dv_all[half_rows:])), CONTEXT, bit
        )
        dk_all = dk_all[:half_rows] + back_k
        dv_all = dv_all[:half_rows] + back_v
    dk_normed = rotate(dk_all, cosine, sine, -1.0)
    key_grad, k_gain_part = norm_backward(k_inputs, k_factor, key_gain, dk_normed)
    q_gain_total, k_gain_total = (by_axis(q_gain_part, CONTEXT), by_axis(k_gain_part, CONTEXT))
    return (
        query_grad.astype(jnp.bfloat16),
        key_grad.astype(jnp.bfloat16),
        dv_all.astype(jnp.bfloat16),
        q_gain_total,
        k_gain_total,
    )


def solution(mesh):
    split = Mesh(
        mesh.devices.reshape(mesh.shape["groups"], 4, 16, 2),
        ("groups", "context_0", "context_1", "context_2"),
    )
    placed = (
        P(GROUPS_CONTEXT, None),
        P(GROUPS_CONTEXT, None),
        P(GROUPS_CONTEXT, None),
        P(GROUPS_CONTEXT, None),
        P(),
        P(),
        P("groups"),
        P("groups"),
    )
    return jax.shard_map(
        body,
        mesh=split,
        in_specs=placed,
        out_specs=(
            P(GROUPS_CONTEXT, None),
            P(GROUPS_CONTEXT, None),
            P(GROUPS_CONTEXT, None),
            P("groups"),
            P("groups"),
        ),
        check_vma=False,
    )
```

profile of v0, /device:TPU:33, one launch (start us, length us, event | category | flops | bytes accessed | tf_op | source)
XLA Modules:
  0.0 238.2 jit_solution(13967253927241340696)
XLA Ops:
  1.4 3.5 %gather_fusion.1 = s32[512]{0:T(512)S(1)} fusion(s32[256]{0:T(256)S(1)} %copy-done.2, s32[1024]{0:T(1024)S(1)} %pad_clamp_fusion.2), kind=kCustom, calls=%fused_computation.1 | custom fusion | bytes 6144 | tf_op jit(solution)/shard_map/jit(_take)/gather | solution.py:111
  9.1 20.5 %collective-permute-start = (bf16[128,1024]{1,0:T(8,128)(2,1)S(1)}, bf16[128,1024]{1,0:T(8,128)(2,1)}, u32[]{:S(2)}, u32[]{:S(2)}) collective-permute-start(bf16[128,1024]{1,0:T(8,128)(2,1)S(1)} %copy.74), channel_id=1, source_target_pairs={{0,1},{1,0},{2,3},{3,2},{4,5},{5,4},{6,7},{7,6},{8,9},{9,8},{10,11... | collective-permute-start | bytes 786440 | tf_op jit(solution)/shard_map/ppermute | solution.py:27
  30.0 3.1 %gather_fusion.2 = s32[512]{0:T(512)S(1)} fusion(s32[16384]{0:T(1024)S(1)} %copy-done, s32[1024]{0:T(1024)S(1)} %get-tuple-element.89), kind=kCustom, calls=%fused_computation.2 | custom fusion | bytes 6144 | tf_op jit(solution)/shard_map/jit(_take)/gather | solution.py:113
  34.8 2.2 fusion.9
  61.2 6.0 %collective-permute-done.3 = bf16[256,1024]{1,0:T(8,128)(2,1)} collective-permute-done((bf16[256,1024]{1,0:T(8,128)(2,1)}, bf16[256,1024]{1,0:T(8,128)(2,1)}, u32[]{:S(2)}, u32[]{:S(2)}) %collective-permute-start.3) | collective-permute-done | bytes 524320 | tf_op jit(solution)/shard_map/ppermute | solution.py:27
  72.4 2.5 %fusion.57 = f32[512,1024]{0,1:T(8,128)} fusion(bf16[128,5,128]{0,2,1:T(8,128)(2,1)} %bitcast.579, f32[5,128]{1,0:T(8,128)S(1)} %get-tuple-element.56, bf16[128,5,128]{0,2,1:T(8,128)(2,1)S(1)} %bitcast.564, pred[128,512]{0,1:T(8,128)(4,1)S(1)} %copy-done.54, bf16[512,1024]{1,0:T(8,128)(2,1)S(1)} %pad_maximum_fusion.2), kind=kOutput, calls=%fused_computation.120 | convolution fusion | flops 169411712 | bytes 790528 | tf_op jit(solution)/shard_map/gqk,qgd->kd/dot_general | solution.py:102
  80.3 2.5 %fusion.134 = (f32[5,128]{1,0:T(8,128)S(1)}, f32[5,128,512]{1,2,0:T(8,128)}) fusion(bf16[128,5,128]{0,2,1:T(8,128)(2,1)} %bitcast.556, pred[128,512]{0,1:T(8,128)(4,1)S(1)} %copy-done.54, bf16[512,1024]{1,0:T(8,128)(2,1)S(1)} %pad_maximum_fusion.2), kind=kOutput, calls=%fused_computation.312 | convolution fusion | flops 85197312 | bytes 1673728 | tf_op jit(solution)/shard_map/sub | solution.py:90
  86.9 2.5 %fusion.135 = (f32[5,128]{1,0:T(8,128)S(1)}, f32[5,128,512]{1,2,0:T(8,128)}) fusion(bf16[128,5,128]{0,2,1:T(8,128)(2,1)} %bitcast.553, pred[128,512]{0,1:T(8,128)(4,1)S(1)} %copy-done.54, bf16[512,1024]{1,0:T(8,128)(2,1)S(1)} %pad_maximum_fusion.2), kind=kOutput, calls=%fused_computation.313 | convolution fusion | flops 85197312 | bytes 1673728 | tf_op jit(solution)/shard_map/sub | solution.py:90
  89.4 1.9 multiply_reduce_fusion.4
  93.6 2.5 %fusion.136 = (f32[5,128]{1,0:T(8,128)S(1)}, f32[5,128,512]{1,2,0:T(8,128)}) fusion(bf16[128,5,128]{0,2,1:T(8,128)(2,1)} %bitcast.550, pred[128,512]{0,1:T(8,128)(4,1)S(1)} %copy-done.54, bf16[512,1024]{1,0:T(8,128)(2,1)S(1)} %pad_maximum_fusion.2), kind=kOutput, calls=%fused_computation.314 | convolution fusion | flops 85197312 | bytes 1673728 | tf_op jit(solution)/shard_map/sub | solution.py:90
  96.1 1.9 multiply_reduce_fusion.3
  100.3 2.5 %fusion.137 = (f32[5,128]{1,0:T(8,128)S(1)}, f32[5,128,512]{1,2,0:T(8,128)}) fusion(bf16[128,5,128]{0,2,1:T(8,128)(2,1)} %bitcast.547, pred[128,512]{0,1:T(8,128)(4,1)S(1)} %copy-done.54, bf16[512,1024]{1,0:T(8,128)(2,1)S(1)} %pad_maximum_fusion.2), kind=kOutput, calls=%fused_computation.315 | convolution fusion | flops 85197312 | bytes 1673728 | tf_op jit(solution)/shard_map/sub | solution.py:90
  107.1 2.5 %fusion.138 = (f32[5,128]{1,0:T(8,128)S(1)}, f32[5,128,512]{1,2,0:T(8,128)}) fusion(bf16[128,5,128]{0,2,1:T(8,128)(2,1)} %bitcast.544, pred[128,512]{0,1:T(8,128)(4,1)S(1)} %copy-done.54, bf16[512,1024]{1,0:T(8,128)(2,1)S(1)} %pad_maximum_fusion.2), kind=kOutput, calls=%fused_computation.316 | convolution fusion | flops 85197312 | bytes 1673728 | tf_op jit(solution)/shard_map/sub | solution.py:90
  113.8 2.5 %fusion.139 = (f32[5,128]{1,0:T(8,128)S(1)}, f32[5,128,512]{1,2,0:T(8,128)}) fusion(bf16[128,5,128]{0,2,1:T(8,128)(2,1)} %bitcast.541, pred[128,512]{0,1:T(8,128)(4,1)S(1)} %copy-done.54, bf16[512,1024]{1,0:T(8,128)(2,1)S(1)} %pad_maximum_fusion.2), kind=kOutput, calls=%fused_computation.317 | convolution fusion | flops 85197312 | bytes 1673728 | tf_op jit(solution)/shard_map/sub | solution.py:90
  116.3 1.9 multiply_reduce_fusion
  120.2 2.1 slice.375
  126.9 3.0 %fusion.17 = (f32[5120]{0:T(1024)S(1)}, f32[128]{0:T(128)S(1)}) fusion(bf16[128,5120]{0,1:T(8,128)(2,1)S(1)} %copy.70, f32[128,40,2,64]{0,3,2,1:T(8,128)S(1)} %pad_maximum_fusion, f32[128]{0:T(128)S(1)} %add_rsqrt_fusion.1, f32[5120]{0:T(1024)S(1)} %copy-done.44), kind=kLoop, calls=%fused_computation.25 | loop fusion | flops 4582272 | bytes 3974144 | tf_op jit(solution)/shard_map/reduce_sum | solution.py:76
  140.5 2.1 slice.374
  143.8 3.5 %fusion.13 = bf16[128,5120]{0,1:T(8,128)(2,1)S(1)} fusion(bf16[128,5120]{0,1:T(8,128)(2,1)S(1)} %copy.70, f32[128,40,2,64]{0,3,2,1:T(8,128)} %copy-done.3, f32[128]{0:T(128)S(1)} %broadcast_multiply_fusion.2, f32[5120]{0:T(1024)S(1)} %copy-done.44, f32[128]{0:T(128)S(1)} %add_rsqrt_fusion.1), kind=kLoop, calls=%fused_computation.21 | loop fusion | flops 5898240 | bytes 5264384 | tf_op jit(solution)/shard_map/convert_element_type | solution.py:171
  152.1 3.1 %collective-permute-done.6 = bf16[256,1024]{0,1:T(8,128)(2,1)S(1)} collective-permute-done((bf16[256,1024]{0,1:T(8,128)(2,1)}, bf16[256,1024]{0,1:T(8,128)(2,1)S(1)}, u32[]{:S(2)}, u32[]{:S(2)}) %collective-permute-start.6) | collective-permute-done | bytes 524320 | tf_op jit(solution)/shard_map/ppermute | solution.py:27
  155.5 2.0 collective-permute-start.7
  160.6 11.0 %all-reduce.1 = (f32[5120]{0:T(1024)S(1)}, f32[1024]{0:T(1024)S(1)}) all-reduce(f32[5120]{0:T(1024)S(1)} %get-tuple-element.15, f32[1024]{0:T(1024)S(1)} %get-tuple-element.17), channel_id=1, replica_groups=mesh['groups'=2,'context_0'=4,'context_1'=16,'context_2'=2] {'context_0'}, use_global_device_ids=true, to_apply=%region_29.30 | all-reduce | flops 6144 | bytes 49152 | tf_op jit(solution)/shard_map/psum | solution.py:40
  171.6 45.1 %all-reduce = (f32[5120]{0:T(1024)S(1)}, f32[1024]{0:T(1024)S(1)}) all-reduce(f32[5120]{0:T(1024)S(1)} %get-tuple-element.21, f32[1024]{0:T(1024)S(1)} %get-tuple-element.22), channel_id=1, replica_groups=mesh['groups'=2,'context_0'=4,'context_1'=16,'context_2'=2] {'context_1'}, use_global_device_ids=true, to_apply=%region_30.31 | all-reduce | flops 6144 | bytes 49152 | tf_op jit(solution)/shard_map/psum | solution.py:40
  216.7 21.5 %all-reduce.2 = (f32[5120]{0:T(1024)}, f32[1024]{0:T(1024)}) all-reduce(f32[5120]{0:T(1024)S(1)} %get-tuple-element.19, f32[1024]{0:T(1024)S(1)} %get-tuple-element.20), channel_id=1, replica_groups=mesh['groups'=2,'context_0'=4,'context_1'=16,'context_2'=2] {'context_2'}, use_global_device_ids=true, to_apply=%region_31.32 | all-reduce | flops 6144 | bytes 49152 | tf_op jit(solution)/shard_map/psum | solution.py:40
  (237 shorter events, 84.9 us)
Async XLA Ops:
  0.6 5.7 %copy-start = (s32[16384]{0:T(1024)S(1)}, s32[16384]{0:T(1024)}, u32[]{:S(2)}) copy-start(s32[16384]{0:T(1024)} %param.14) | copy-start | bytes 196612
  1.4 6.1 %copy-start.43 = (bf16[128,1024]{1,0:T(8,128)(2,1)S(1)}, bf16[128,1024]{1,0:T(8,128)(2,1)}, u32[]{:S(2)}) copy-start(bf16[128,1024]{1,0:T(8,128)(2,1)} %param.9) | copy-start | bytes 786436
  4.9 3.8 %copy-start.55 = (f32[1024]{0:T(1024)S(1)}, f32[1024]{0:T(1024)}, u32[]{:S(2)}) copy-start(f32[1024]{0:T(1024)} %param.13) | copy-start | bytes 12292
  8.6 21.0 %copy-start.20 = (bf16[128,1024]{1,0:T(8,128)(2,1)S(1)}, bf16[128,1024]{1,0:T(8,128)(2,1)}, u32[]{:S(2)}) copy-start(bf16[128,1024]{1,0:T(8,128)(2,1)} %param.10) | copy-start | bytes 786436
  9.0 24.3 %copy-start.12 = (bf16[128,5120]{1,0:T(8,128)(2,1)S(1)}, bf16[128,5120]{1,0:T(8,128)(2,1)}, u32[]{:S(2)}) copy-start(bf16[128,5120]{1,0:T(8,128)(2,1)} %param.8) | copy-start | bytes 3932164
  9.1 31.4 %collective-permute-start = (bf16[128,1024]{1,0:T(8,128)(2,1)S(1)}, bf16[128,1024]{1,0:T(8,128)(2,1)}, u32[]{:S(2)}, u32[]{:S(2)}) collective-permute-start(bf16[128,1024]{1,0:T(8,128)(2,1)S(1)} %copy.74), channel_id=1, source_target_pairs={{0,1},{1,0},{2,3},{3,2},{4,5},{5,4},{6,7},{7,6},{8,9},{9,8},{10,11... | collective-permute-start | bytes 786440 | tf_op jit(solution)/shard_map/ppermute | solution.py:27
  29.7 17.9 %collective-permute-start.2 = (bf16[128,1024]{1,0:T(8,128)(2,1)S(1)}, bf16[128,1024]{1,0:T(8,128)(2,1)}, u32[]{:S(2)}, u32[]{:S(2)}) collective-permute-start(bf16[128,1024]{1,0:T(8,128)(2,1)S(1)} %copy-done.20), channel_id=1, source_target_pairs={{0,1},{1,0},{2,3},{3,2},{4,5},{5,4},{6,7},{7,6},{8,9},{9,8},{10,11... | collective-permute-start | bytes 786440 | tf_op jit(solution)/shard_map/ppermute | solution.py:27
  42.3 16.1 %collective-permute-start.1 = (bf16[256,1024]{1,0:T(8,128)(2,1)}, bf16[256,1024]{1,0:T(8,128)(2,1)}, u32[]{:S(2)}, u32[]{:S(2)}) collective-permute-start(bf16[256,1024]{1,0:T(8,128)(2,1)} %pad_maximum_fusion.3), channel_id=1, source_target_pairs={{0,2},{2,0},{1,3},{3,1},{4,6},{6,4},{5,7},{7,5},{8,10},{10,8},{9,1... | collective-permute-start | bytes 1572872 | tf_op jit(solution)/shard_map/ppermute | solution.py:27
  47.5 5.1 %copy-start.25 = (bf16[128,640]{1,0:T(8,128)(2,1)S(1)}, bf16[128,640]{1,0:T(8,128)(2,1)}, u32[]{:S(2)}) copy-start(bf16[128,640]{1,0:T(8,128)(2,1)} %get-tuple-element.45) | copy-start | bytes 491524
  47.5 5.9 %copy-start.24 = (bf16[128,640]{1,0:T(8,128)(2,1)S(1)}, bf16[128,640]{1,0:T(8,128)(2,1)}, u32[]{:S(2)}) copy-start(bf16[128,640]{1,0:T(8,128)(2,1)} %get-tuple-element.44) | copy-start | bytes 491524
  47.5 6.7 %copy-start.23 = (bf16[128,640]{1,0:T(8,128)(2,1)S(1)}, bf16[128,640]{1,0:T(8,128)(2,1)}, u32[]{:S(2)}) copy-start(bf16[128,640]{1,0:T(8,128)(2,1)} %get-tuple-element.43) | copy-start | bytes 491524
  47.5 7.5 %copy-start.22 = (bf16[128,640]{1,0:T(8,128)(2,1)S(1)}, bf16[128,640]{1,0:T(8,128)(2,1)}, u32[]{:S(2)}) copy-start(bf16[128,640]{1,0:T(8,128)(2,1)} %get-tuple-element.42) | copy-start | bytes 491524
  47.5 8.3 %copy-start.21 = (bf16[128,640]{1,0:T(8,128)(2,1)S(1)}, bf16[128,640]{1,0:T(8,128)(2,1)}, u32[]{:S(2)}) copy-start(bf16[128,640]{1,0:T(8,128)(2,1)} %get-tuple-element.41) | copy-start | bytes 491524
  49.4 17.8 %collective-permute-start.3 = (bf16[256,1024]{1,0:T(8,128)(2,1)}, bf16[256,1024]{1,0:T(8,128)(2,1)}, u32[]{:S(2)}, u32[]{:S(2)}) collective-permute-start(bf16[256,1024]{1,0:T(8,128)(2,1)} %pad_maximum_fusion.4), channel_id=1, source_target_pairs={{0,2},{2,0},{1,3},{3,1},{4,6},{6,4},{5,7},{7,5},{8,10},{10,8},{9,1... | collective-permute-start | bytes 1572872 | tf_op jit(solution)/shard_map/ppermute | solution.py:27
  56.7 2.9 %copy-start.54 = (pred[128,512]{0,1:T(8,128)(4,1)S(1)}, pred[128,512]{0,1:T(8,128)(4,1)}, u32[]{:S(2)}) copy-start(pred[128,512]{0,1:T(8,128)(4,1)} %compare_and_fusion) | copy-start | bytes 196612
  59.6 9.5 %copy-start.53 = (bf16[128,640]{0,1:T(8,128)(2,1)S(1)}, bf16[128,640]{0,1:T(8,128)(2,1)}, u32[]{:S(2)}) copy-start(bf16[128,640]{0,1:T(8,128)(2,1)} %copy.190) | copy-start | bytes 491524
  122.3 26.4 %collective-permute-start.4 = (bf16[256,1024]{0,1:T(8,128)(2,1)}, bf16[256,1024]{0,1:T(8,128)(2,1)}, u32[]{:S(2)}, u32[]{:S(2)}) collective-permute-start(bf16[256,1024]{0,1:T(8,128)(2,1)} %slice.375), channel_id=1, source_target_pairs={{0,2},{2,0},{1,3},{3,1},{4,6},{6,4},{5,7},{7,5},{8,10},{10,8},{9,1... | collective-permute-start | bytes 1572872 | tf_op jit(solution)/shard_map/ppermute | solution.py:27
  126.9 3.0 %copy-start.40 = (bf16[128,640]{0,1:T(8,128)(2,1)S(1)}, bf16[128,640]{0,1:T(8,128)(2,1)}, u32[]{:S(2)}) copy-start(bf16[128,640]{0,1:T(8,128)(2,1)} %get-tuple-element.39) | copy-start | bytes 491524
  126.9 3.0 %copy-start.47 = (bf16[128,640]{0,1:T(8,128)(2,1)S(1)}, bf16[128,640]{0,1:T(8,128)(2,1)}, u32[]{:S(2)}) copy-start(bf16[128,640]{0,1:T(8,128)(2,1)} %copy.191) | copy-start | bytes 491524
  142.6 12.7 %collective-permute-start.6 = (bf16[256,1024]{0,1:T(8,128)(2,1)}, bf16[256,1024]{0,1:T(8,128)(2,1)S(1)}, u32[]{:S(2)}, u32[]{:S(2)}) collective-permute-start(bf16[256,1024]{0,1:T(8,128)(2,1)} %slice.374), channel_id=1, source_target_pairs={{0,2},{2,0},{1,3},{3,1},{4,6},{6,4},{5,7},{7,5},{8,10},{10,8},{9,1... | collective-permute-start | bytes 1572872 | tf_op jit(solution)/shard_map/ppermute | solution.py:27
  148.8 6.5 %copy-start.19 = (f32[512,1024]{0,1:T(8,128)S(1)}, f32[512,1024]{0,1:T(8,128)}, u32[]{:S(2)}) copy-start(f32[512,1024]{0,1:T(8,128)} %fusion.50) | copy-start | bytes 6291460
  150.4 7.1 %collective-permute-start.5 = (bf16[128,1024]{0,1:T(8,128)(2,1)S(1)}, bf16[128,1024]{0,1:T(8,128)(2,1)S(1)}, u32[]{:S(2)}, u32[]{:S(2)}) collective-permute-start(bf16[128,1024]{0,1:T(8,128)(2,1)S(1)} %slice.377), channel_id=1, source_target_pairs={{0,1},{1,0},{2,3},{3,2},{4,5},{5,4},{6,7},{7,6},{8,9},{9,8},{10,11... | collective-permute-start | bytes 786440 | tf_op jit(solution)/shard_map/ppermute | solution.py:27
  155.5 3.2 %collective-permute-start.7 = (bf16[128,1024]{0,1:T(8,128)(2,1)S(1)}, bf16[128,1024]{0,1:T(8,128)(2,1)S(1)}, u32[]{:S(2)}, u32[]{:S(2)}) collective-permute-start(bf16[128,1024]{0,1:T(8,128)(2,1)S(1)} %slice.376), channel_id=1, source_target_pairs={{0,1},{1,0},{2,3},{3,2},{4,5},{5,4},{6,7},{7,6},{8,9},{9,8},{10,11... | collective-permute-start | bytes 786440 | tf_op jit(solution)/shard_map/ppermute | solution.py:27
  158.7 79.5 %copy-start.1 = (s32[16384]{0:T(1024)S(1)}, s32[16384]{0:T(1024)}, u32[]{:S(2)}) copy-start(s32[16384]{0:T(1024)} %param.14) | copy-start | bytes 196612
  (40 other events, 61.7 us)
where the time goes:
time: 239 us; the launch traced here: 238 us
  blocking collectives  77.5 us (32%)
  matrix products  60.7 us (25%)
  local copies, waits for them, and re-layouts  39.1 us (16%)
  starting transfers between devices  27.5 us (12%)
  other arithmetic  22.1 us (9%)
  waiting for transfers between devices  9.75 us (4%)
    psum x3, blocking collectives, by_axis(): array = lax.psum(array, axis)  77.5 us
    ppermute x8, starting transfers between devices, swapped(): return lax.ppermute(block, axis, route)  27.5 us
    unnamed x134, local copies, waits for them, and re-layouts  21.6 us
    sub x8, matrix products, head_gradients(): expo = jnp.exp(scores - row_max)  18.1 us
    dot_general x8, matrix products, head_gradients(): jnp.einsum('qgd,kd->gqk', grad_heads, value_rows, preferred_element_type=...  15 us
    dot_general x8, matrix products, head_gradients(): jnp.einsum('gqk,qgd->kd', probs_low, grad_heads, preferred_element_type=j...  13 us
    ppermute x8, waiting for transfers between devices, swapped(): return lax.ppermute(block, axis, route)  9.75 us
    dot_general x8, matrix products, head_gradients(): jnp.einsum('gqk,qgd->kd', dscores, query_heads, preferred_element_type=jn...  8.41 us
  transfers between devices with their start and end apart: 8, of which 3 were waited for; matrix products, arithmetic and copies ran while one was open for 22% of the time, Pallas kernels for 0%

commit v1 on v0

--- a/solution.py
+++ b/solution.py
@@ -37,7 +37,8 @@
 
 def by_axis(array, axes):
     for axis in axes:
-        array = lax.psum(array, axis)
+        pieces = lax.all_gather(array, axis, axis=0, tiled=False)
+        array = pieces.sum(axis=0)
     return array
 
 

time: 239 us -> 258 us (1.079)
  blocking collectives: 77.5 us -> 87.3 us
  matrix products: 60.7 us -> 68.4 us
  other arithmetic: 22.1 us -> 26.1 us
  starting transfers between devices: 27.5 us -> 24.6 us
    all_gather x0 -> x6, blocking collectives: none -> 87.3 us  [by_axis(): pieces = lax.all_gather(array, axis, axis=0, tiled=False)]
    psum x3 -> x0, blocking collectives: 77.5 us -> none  [by_axis(): array = lax.psum(array, axis)]
    dot_general x8, matrix products: 13 us -> 19.6 us  [head_gradients(): jnp.einsum('gqk,qgd->kd', probs_low, grad_heads, preferred_element_type=j...]
    dot_general x8, matrix products: 6.18 us -> 12.4 us  [head_gradients(): jnp.einsum('gqk,kd->qgd', dscores, key_rows, preferred_element_type=jnp.f...]
    dot_general x8, matrix products: 8.41 us -> 3.47 us  [head_gradients(): jnp.einsum('gqk,qgd->kd', dscores, query_heads, preferred_element_type=jn...]
    ppermute x8, starting transfers between devices: 27.5 us -> 24.6 us  [swapped(): return lax.ppermute(block, axis, route)]
    unnamed x134 -> x190, local copies, waits for them, and re-layouts: 21.6 us -> 24 us
  transfers between devices with their start and end apart: 8 -> 8, of which waited for: 3 -> 2; matrix products, arithmetic and copies ran while one was open for 22% -> 22% of each run, Pallas kernels for 0% -> 0%
where the time goes in v1:
time: 258 us; the launch traced here: 256 us
  blocking collectives  87.3 us (34%)
  matrix products  68.4 us (27%)
  local copies, waits for them, and re-layouts  41 us (16%)
  other arithmetic  26.1 us (10%)
  starting transfers between devices  24.6 us (10%)
  waiting for transfers between devices  7.2 us (3%)
    all_gather x6, blocking collectives, by_axis(): pieces = lax.all_gather(array, axis, axis=0, tiled=False)  87.3 us
    ppermute x8, starting transfers between devices, swapped(): return lax.ppermute(block, axis, route)  24.6 us
    unnamed x190, local copies, waits for them, and re-layouts  24 us
    dot_general x8, matrix products, head_gradients(): jnp.einsum('gqk,qgd->kd', probs_low, grad_heads, preferred_element_type=j...  19.6 us
    sub x8, matrix products, head_gradients(): expo = jnp.exp(scores - row_max)  18 us
    dot_general x8, matrix products, head_gradients(): jnp.einsum('qgd,kd->gqk', grad_heads, value_rows, preferred_element_type=...  15 us
    dot_general x8, matrix products, head_gradients(): jnp.einsum('gqk,kd->qgd', dscores, key_rows, preferred_element_type=jnp.f...  12.4 us
    ppermute x8, waiting for transfers between devices, swapped(): return lax.ppermute(block, axis, route)  7.2 us
  transfers between devices with their start and end apart: 8, of which 2 were waited for; matrix products, arithmetic and copies ran while one was open for 22% of the time, Pallas kernels for 0%

profile of v1, /device:TPU:33, one launch (start us, length us, event | category | flops | bytes accessed | tf_op | source)
XLA Modules:
  0.0 256.4 jit_solution(13349108493785950345)
XLA Ops:
  2.7 3.5 %gather_fusion.1 = s32[512]{0:T(512)S(1)} fusion(s32[256]{0:T(256)S(1)} %copy-done.2, s32[1024]{0:T(1024)S(1)} %pad_clamp_fusion.2), kind=kCustom, calls=%fused_computation.1 | custom fusion | bytes 6144 | tf_op jit(solution)/shard_map/jit(_take)/gather | solution.py:112
  9.7 20.5 %collective-permute-start = (bf16[128,1024]{1,0:T(8,128)(2,1)S(1)}, bf16[128,1024]{1,0:T(8,128)(2,1)}, u32[]{:S(2)}, u32[]{:S(2)}) collective-permute-start(bf16[128,1024]{1,0:T(8,128)(2,1)S(1)} %copy.202), channel_id=1, source_target_pairs={{0,1},{1,0},{2,3},{3,2},{4,5},{5,4},{6,7},{7,6},{8,9},{9,8},{10,11... | collective-permute-start | bytes 786440 | tf_op jit(solution)/shard_map/ppermute | solution.py:27
  35.7 3.1 %gather_fusion.2 = s32[512]{0:T(512)S(1)} fusion(s32[16384]{0:T(1024)S(1)} %copy-done, s32[1024]{0:T(1024)S(1)} %get-tuple-element.93), kind=kCustom, calls=%fused_computation.2 | custom fusion | bytes 6144 | tf_op jit(solution)/shard_map/jit(_take)/gather | solution.py:114
  61.8 6.6 %collective-permute-done.3 = bf16[256,1024]{1,0:T(8,128)(2,1)} collective-permute-done((bf16[256,1024]{1,0:T(8,128)(2,1)}, bf16[256,1024]{1,0:T(8,128)(2,1)}, u32[]{:S(2)}, u32[]{:S(2)}) %collective-permute-start.3) | collective-permute-done | bytes 524320 | tf_op jit(solution)/shard_map/ppermute | solution.py:27
  74.4 2.5 fusion.57
  82.3 2.5 fusion.134
  88.2 2.5 fusion.135
  95.6 2.5 fusion.136
  102.9 2.5 fusion.137
  110.3 2.5 fusion.138
  117.7 2.5 fusion.139
  126.5 3.2 %fusion.17 = (f32[5120]{0:T(1024)S(1)}, f32[128]{0:T(128)S(1)}) fusion(bf16[128,5120]{0,1:T(8,128)(2,1)S(1)} %copy.198, f32[128,40,2,64]{0,3,2,1:T(8,128)S(1)} %pad_maximum_fusion, f32[128]{0:T(128)S(1)} %copy-done.76, f32[5120]{0:T(1024)S(1)} %copy-done.61), kind=kLoop, calls=%fused_computation.25 | loop fusion | flops 4582272 | bytes 3974144 | tf_op jit(solution)/shard_map/reduce_sum | solution.py:77
  138.2 2.5 fusion.55
  140.7 2.4 fusion.54
  143.1 2.4 fusion.53
  145.6 2.5 fusion.52
  148.0 2.4 fusion.51
  156.1 3.5 %fusion.13 = bf16[128,5120]{0,1:T(8,128)(2,1)S(1)} fusion(bf16[128,5120]{0,1:T(8,128)(2,1)S(1)} %copy.198, f32[128,40,2,64]{0,3,2,1:T(8,128)} %copy-done.3, f32[128]{0:T(128)S(1)} %broadcast_multiply_fusion.2, f32[5120]{0:T(1024)S(1)} %copy-done.61, f32[128]{0:T(128)S(1)} %copy-done.76), kind=kLoop, calls=%fused_computation.21 | loop fusion | flops 5898240 | bytes 5264384 | tf_op jit(solution)/shard_map/convert_element_type | solution.py:172
  161.1 9.0 %all-gather = f32[20480]{0:T(1024)S(1)} all-gather(f32[5120]{0:T(1024)S(1)} %get-tuple-element.25), channel_id=2, replica_groups=mesh['groups'=2,'context_0'=4,'context_1'=16,'context_2'=2] {'context_0'}, dimensions={0}, use_global_device_ids=true | all-gather | bytes 102400 | tf_op jit(solution)/shard_map/all_gather | solution.py:40
  170.2 25.0 %all-gather.1 = f32[81920]{0:T(1024)S(1)} all-gather(f32[5120]{0:T(1024)S(1)} %reduce_sum.273), channel_id=3, replica_groups=mesh['groups'=2,'context_0'=4,'context_1'=16,'context_2'=2] {'context_1'}, dimensions={0}, use_global_device_ids=true | all-gather | bytes 348160 | tf_op jit(solution)/shard_map/all_gather | solution.py:40
  195.3 13.1 %all-gather.2 = f32[10240]{0:T(1024)S(1)} all-gather(f32[5120]{0:T(1024)S(1)} %reduce_sum.274), channel_id=4, replica_groups=mesh['groups'=2,'context_0'=4,'context_1'=16,'context_2'=2] {'context_2'}, dimensions={0}, use_global_device_ids=true | all-gather | bytes 61440 | tf_op jit(solution)/shard_map/all_gather | solution.py:40
  215.4 9.1 %all-gather.3 = f32[4096]{0:T(1024)S(1)} all-gather(f32[1024]{0:T(1024)S(1)} %get-tuple-element.27), channel_id=5, replica_groups=mesh['groups'=2,'context_0'=4,'context_1'=16,'context_2'=2] {'context_0'}, dimensions={0}, use_global_device_ids=true | all-gather | bytes 20480 | tf_op jit(solution)/shard_map/all_gather | solution.py:40
  224.6 19.4 %all-gather.4 = f32[16384]{0:T(1024)S(1)} all-gather(f32[1024]{0:T(1024)S(1)} %reduce_sum.277), channel_id=6, replica_groups=mesh['groups'=2,'context_0'=4,'context_1'=16,'context_2'=2] {'context_1'}, dimensions={0}, use_global_device_ids=true | all-gather | bytes 69632 | tf_op jit(solution)/shard_map/all_gather | solution.py:40
  244.1 11.7 %all-gather.5 = f32[2048]{0:T(1024)S(1)} all-gather(f32[1024]{0:T(1024)S(1)} %reduce_sum.278), channel_id=7, replica_groups=mesh['groups'=2,'context_0'=4,'context_1'=16,'context_2'=2] {'context_2'}, dimensions={0}, use_global_device_ids=true | all-gather | bytes 12288 | tf_op jit(solution)/shard_map/all_gather | solution.py:40
  (308 shorter events, 97.1 us)
Async XLA Ops:
  0.6 5.7 %copy-start = (s32[16384]{0:T(1024)S(1)}, s32[16384]{0:T(1024)}, u32[]{:S(2)}) copy-start(s32[16384]{0:T(1024)} %param.14) | copy-start | bytes 196612
  0.7 5.5 %copy-start.82 = (s32[128]{0:T(128)}, s32[128]{0:T(128)S(1)}, u32[]{:S(2)}) copy-start(s32[128]{0:T(128)S(1)} %and_select_fusion.7) | copy-start | bytes 1540
  0.7 5.6 %copy-start.77 = (s32[128]{0:T(128)}, s32[128]{0:T(128)S(1)}, u32[]{:S(2)}) copy-start(s32[128]{0:T(128)S(1)} %and_select_fusion.10) | copy-start | bytes 1540
  2.7 5.4 %copy-start.59 = (bf16[128,1024]{1,0:T(8,128)(2,1)S(1)}, bf16[128,1024]{1,0:T(8,128)(2,1)}, u32[]{:S(2)}) copy-start(bf16[128,1024]{1,0:T(8,128)(2,1)} %param.9) | copy-start | bytes 786436
  2.7 6.5 %copy-start.72 = (f32[1024]{0:T(1024)S(1)}, f32[1024]{0:T(1024)}, u32[]{:S(2)}) copy-start(f32[1024]{0:T(1024)} %param.13) | copy-start | bytes 12292
  9.2 21.0 %copy-start.35 = (bf16[128,1024]{1,0:T(8,128)(2,1)S(1)}, bf16[128,1024]{1,0:T(8,128)(2,1)}, u32[]{:S(2)}) copy-start(bf16[128,1024]{1,0:T(8,128)(2,1)} %param.10) | copy-start | bytes 786436
  9.2 21.4 %copy-start.26 = (bf16[128,5120]{1,0:T(8,128)(2,1)S(1)}, bf16[128,5120]{1,0:T(8,128)(2,1)}, u32[]{:S(2)}) copy-start(bf16[128,5120]{1,0:T(8,128)(2,1)} %param.8) | copy-start | bytes 3932164
  9.7 32.3 %copy-start.14 = (bf16[128,1024]{1,0:T(8,128)(2,1)}, bf16[128,1024]{1,0:T(8,128)(2,1)S(1)}, u32[]{:S(2)}) copy-start(bf16[128,1024]{1,0:T(8,128)(2,1)S(1)} %copy.202) | copy-start | bytes 786436
  9.7 32.3 %collective-permute-start = (bf16[128,1024]{1,0:T(8,128)(2,1)S(1)}, bf16[128,1024]{1,0:T(8,128)(2,1)}, u32[]{:S(2)}, u32[]{:S(2)}) collective-permute-start(bf16[128,1024]{1,0:T(8,128)(2,1)S(1)} %copy.202), channel_id=1, source_target_pairs={{0,1},{1,0},{2,3},{3,2},{4,5},{5,4},{6,7},{7,6},{8,9},{9,8},{10,11... | collective-permute-start | bytes 786440 | tf_op jit(solution)/shard_map/ppermute | solution.py:27
  30.3 18.8 %collective-permute-start.2 = (bf16[128,1024]{1,0:T(8,128)(2,1)S(1)}, bf16[128,1024]{1,0:T(8,128)(2,1)}, u32[]{:S(2)}, u32[]{:S(2)}) collective-permute-start(bf16[128,1024]{1,0:T(8,128)(2,1)S(1)} %copy-done.35), channel_id=1, source_target_pairs={{0,1},{1,0},{2,3},{3,2},{4,5},{5,4},{6,7},{7,6},{8,9},{9,8},{10,11... | collective-permute-start | bytes 786440 | tf_op jit(solution)/shard_map/ppermute | solution.py:27
  39.2 78.5 %copy-start.71 = (pred[128,512]{0,1:T(8,128)(4,1)}, pred[128,512]{0,1:T(8,128)(4,1)S(1)}, u32[]{:S(2)}) copy-start(pred[128,512]{0,1:T(8,128)(4,1)S(1)} %compare_and_fusion) | copy-start | bytes 196612
  43.8 15.2 %collective-permute-start.1 = (bf16[256,1024]{1,0:T(8,128)(2,1)}, bf16[256,1024]{1,0:T(8,128)(2,1)}, u32[]{:S(2)}, u32[]{:S(2)}) collective-permute-start(bf16[256,1024]{1,0:T(8,128)(2,1)} %pad_maximum_fusion.3), channel_id=1, source_target_pairs={{0,2},{2,0},{1,3},{3,1},{4,6},{6,4},{5,7},{7,5},{8,10},{10,8},{9,1... | collective-permute-start | bytes 1572872 | tf_op jit(solution)/shard_map/ppermute | solution.py:27
  49.0 5.8 %copy-start.38 = (bf16[128,640]{1,0:T(8,128)(2,1)S(1)}, bf16[128,640]{1,0:T(8,128)(2,1)}, u32[]{:S(2)}) copy-start(bf16[128,640]{1,0:T(8,128)(2,1)} %get-tuple-element.47) | copy-start | bytes 491524
  49.0 6.6 %copy-start.37 = (bf16[128,640]{1,0:T(8,128)(2,1)S(1)}, bf16[128,640]{1,0:T(8,128)(2,1)}, u32[]{:S(2)}) copy-start(bf16[128,640]{1,0:T(8,128)(2,1)} %get-tuple-element.46) | copy-start | bytes 491524
  49.0 7.4 %copy-start.36 = (bf16[128,640]{1,0:T(8,128)(2,1)S(1)}, bf16[128,640]{1,0:T(8,128)(2,1)}, u32[]{:S(2)}) copy-start(bf16[128,640]{1,0:T(8,128)(2,1)} %get-tuple-element.45) | copy-start | bytes 491524
  50.9 8.0 %copy-start.15 = (bf16[128,1024]{1,0:T(8,128)(2,1)S(1)}, bf16[128,1024]{1,0:T(8,128)(2,1)}, u32[]{:S(2)}) copy-start(bf16[128,1024]{1,0:T(8,128)(2,1)} %copy-done.14) | copy-start | bytes 786436
  50.9 17.4 %collective-permute-start.3 = (bf16[256,1024]{1,0:T(8,128)(2,1)}, bf16[256,1024]{1,0:T(8,128)(2,1)}, u32[]{:S(2)}, u32[]{:S(2)}) collective-permute-start(bf16[256,1024]{1,0:T(8,128)(2,1)} %pad_maximum_fusion.4), channel_id=1, source_target_pairs={{0,2},{2,0},{1,3},{3,1},{4,6},{6,4},{5,7},{7,5},{8,10},{10,8},{9,1... | collective-permute-start | bytes 1572872 | tf_op jit(solution)/shard_map/ppermute | solution.py:27
  60.2 22.2 %copy-start.12 = (bf16[512,1024]{1,0:T(8,128)(2,1)}, bf16[512,1024]{1,0:T(8,128)(2,1)S(1)}, u32[]{:S(2)}) copy-start(bf16[512,1024]{1,0:T(8,128)(2,1)S(1)} %pad_maximum_fusion.2) | copy-start | bytes 3145732
  60.2 10.1 %copy-start.70 = (bf16[128,640]{0,1:T(8,128)(2,1)S(1)}, bf16[128,640]{0,1:T(8,128)(2,1)}, u32[]{:S(2)}) copy-start(bf16[128,640]{0,1:T(8,128)(2,1)} %copy.318) | copy-start | bytes 491524
  135.5 73.6 %collective-permute-start.4 = (bf16[256,1024]{0,1:T(8,128)(2,1)}, bf16[256,1024]{0,1:T(8,128)(2,1)}, u32[]{:S(2)}, u32[]{:S(2)}) collective-permute-start(bf16[256,1024]{0,1:T(8,128)(2,1)} %slice.375), channel_id=1, source_target_pairs={{0,2},{2,0},{1,3},{3,1},{4,6},{6,4},{5,7},{7,5},{8,10},{10,8},{9,1... | collective-permute-start | bytes 1572872 | tf_op jit(solution)/shard_map/ppermute | solution.py:27
  155.0 56.2 %collective-permute-start.6 = (bf16[256,1024]{0,1:T(8,128)(2,1)}, bf16[256,1024]{0,1:T(8,128)(2,1)S(1)}, u32[]{:S(2)}, u32[]{:S(2)}) collective-permute-start(bf16[256,1024]{0,1:T(8,128)(2,1)} %slice.374), channel_id=1, source_target_pairs={{0,2},{2,0},{1,3},{3,1},{4,6},{6,4},{5,7},{7,5},{8,10},{10,8},{9,1... | collective-permute-start | bytes 1572872 | tf_op jit(solution)/shard_map/ppermute | solution.py:27
  210.7 1.7 collective-permute-start.5
  211.4 3.1 %collective-permute-start.7 = (bf16[128,1024]{0,1:T(8,128)(2,1)S(1)}, bf16[128,1024]{0,1:T(8,128)(2,1)S(1)}, u32[]{:S(2)}, u32[]{:S(2)}) collective-permute-start(bf16[128,1024]{0,1:T(8,128)(2,1)S(1)} %slice.376), channel_id=1, source_target_pairs={{0,1},{1,0},{2,3},{3,2},{4,5},{5,4},{6,7},{7,6},{8,9},{9,8},{10,11... | collective-permute-start | bytes 786440 | tf_op jit(solution)/shard_map/ppermute | solution.py:27
  213.5 42.9 %copy-start.1 = (s32[16384]{0:T(1024)S(1)}, s32[16384]{0:T(1024)}, u32[]{:S(2)}) copy-start(s32[16384]{0:T(1024)} %param.14) | copy-start | bytes 196612
  (68 other events, 141.2 us)
